TPU v7x, 128 devices: a whole 4x4x4 slice. The times are simulated.
128 devices in a mesh: gx: 8 (over x, y_hi), gy: 16 (over y_lo, z, core).
Axes of the slice: x: 4, y: 4 (y_hi: 2, y_lo: 2; y = y_hi * 2 + y_lo), z: 4, core: 2. Of those that a mesh axis runs over, the one named last changes fastest.
Arguments:
- species: float32 [24, 128, 256, 128], P(None, 'gx', 'gy'), may hold values from -6 to 6
- diffusivity: float32 [128, 256, 128], P('gx', 'gy'), may hold values from 0.5 to 2
- lewis_number: float32 [24], replicated, may hold values from 0.5 to 2
- velocity: float32 [3, 128, 256, 128], P(None, 'gx', 'gy'), may hold values from -6 to 6
- layer_one: bfloat16 [1600, 24], replicated, may hold values from -1.25 to 1.25
- layer_two: bfloat16 [800, 1600], replicated, may hold values from -0.15625 to 0.15625
- layer_three: bfloat16 [400, 800], replicated, may hold values from -0.21875 to 0.21875
- layer_four: bfloat16 [24, 400], replicated, may hold values from -0.3125 to 0.3125
- heat_release: float32 [24], replicated, may hold values from -3 to 3
- react_index: int32 [8, 16, 4096], P('gx', 'gy'), may hold values from 0 to 32767, as said below
- react_count: int32 [8, 16], P('gx', 'gy'), may hold values from 1 to 4096, as said below
Outputs:
- species_out: float32 [24, 128, 256, 128], P(None, 'gx', 'gy')
- velocity_out: float32 [3, 128, 256, 128], P(None, 'gx', 'gy')
Inputs may be any that keep to these rules, and one draw needn't show every extreme that they name: `react_index`: within each device's list the 4096 numbers are distinct cells of that device; slots from react_count on are padding. `react_count`: in every row of devices along gy the counts rounded up to whole blocks of 128 add up to at most 128, exactly that in some row; every such row has a device whose list is full.
All inputs are finite; a program needn't handle non-finite values.
Results may differ from a plain program's by a relative error of at most 0.00053.
Values may be sent and summed in bfloat16 or wider, within the bound.
A program may use at most 128 MiB of HBM per device.

v0:
```python
import jax
import jax.numpy as jnp
from jax import lax
from jax.sharding import PartitionSpec as P

SUBSTEPS = 2
BLOCK = 128


diffuse_step = 0.03
react_step = 0.5


def in_one_piece(arrays, axis, split_dim, concat_dim, along):
    both = jnp.concatenate(arrays, axis=along)
    filled, at, finished = (
        lax.all_to_all(both, axis, split_axis=split_dim, concat_axis=concat_dim, tiled=True),
        0,
        [],
    )
    for a in arrays:
        finished.append(lax.slice_in_dim(filled, at, at + a.shape[along], axis=along))
        at += a.shape[along]
    return tuple(finished)


def extended(value, sides, width):
    edges = {}
    for axis, dim in sides:
        peers, length = (lax.axis_size(axis), value.shape[dim])
        up = [(i, (i + 1) % peers) for i in range(peers)]
        last = lax.slice_in_dim(value, length - width, length, axis=dim)
        leading = lax.slice_in_dim(value, 0, width, axis=dim)
        edges[dim] = (
            lax.ppermute(last, axis, up),
            lax.ppermute(leading, axis, [(b, a) for a, b in up]),
        )
    done = []
    for _, dim in sides:
        low, high = edges[dim]
        around = [(width, width) if d in done else (0, 0) for d in range(value.ndim)]
        value = jnp.concatenate([jnp.pad(low, around), value, jnp.pad(high, around)], axis=dim)
        done.append(dim)
    return value


def from_behind(value, axis, by):
    peers = lax.axis_size(axis)
    return lax.ppermute(value, axis, [(i, (i + by) % peers) for i in range(peers)])


def diffuse(padded, coeffs):
    center = padded[:, 1:-1, 1:-1, :]
    middle = coeffs[:, 1:-1, 1:-1, :]
    east_flux = 0.5 * (middle + coeffs[:, 2:, 1:-1, :]) * (padded[:, 2:, 1:-1, :] - center)
    west_flux = 0.5 * (coeffs[:, :-2, 1:-1, :] + middle) * (center - padded[:, :-2, 1:-1, :])
    north_flux = 0.5 * (middle + coeffs[:, 1:-1, 2:, :]) * (padded[:, 1:-1, 2:, :] - center)
    south_flux = 0.5 * (coeffs[:, 1:-1, :-2, :] + middle) * (center - padded[:, 1:-1, :-2, :])
    upper_flux = 0.5 * (middle + jnp.roll(middle, -1, 3)) * (jnp.roll(center, -1, 3) - center)
    lower_flux = 0.5 * (jnp.roll(middle, 1, 3) + middle) * (center - jnp.roll(center, 1, 3))
    updated = center + diffuse_step * (
        east_flux - west_flux + (north_flux - south_flux) + (upper_flux - lower_flux)
    )
    return (updated, middle)


def network(blocks, first, second, third, fourth):
    hidden = jax.nn.silu(
        jnp.einsum("fs,bsr->bfr", first, blocks, preferred_element_type=jnp.float32)
    ).astype(jnp.bfloat16)
    hidden = jax.nn.silu(
        jnp.einsum("gf,bfr->bgr", second, hidden, preferred_element_type=jnp.float32)
    ).astype(jnp.bfloat16)
    hidden = jax.nn.silu(
        jnp.einsum("hg,bgr->bhr", third, hidden, preferred_element_type=jnp.float32)
    ).astype(jnp.bfloat16)
    return jnp.einsum("sh,bhr->bsr", fourth, hidden, preferred_element_type=jnp.float32).astype(
        jnp.bfloat16
    )


def tables(length):
    counter = jnp.arange(length, dtype=jnp.int32)
    phase = counter[:, None] * counter[None, :] % length
    angle = phase.astype(jnp.float32) * (2.0 * jnp.pi / length)
    return (jnp.cos(angle), jnp.sin(angle))


def apply_table(values, matrix, axis):
    product = jnp.tensordot(values, matrix, axes=([axis], [0]), precision=lax.Precision.HIGHEST)
    return jnp.moveaxis(product, -1, axis)


def transform(pair, axis, length, inverse):
    cosine, sine = tables(length)
    real_part, imag_part = pair
    real_cos = apply_table(real_part, cosine, axis)
    real_sin = apply_table(real_part, sine, axis)
    imag_cos = apply_table(imag_part, cosine, axis)
    imag_sin = apply_table(imag_part, sine, axis)
    if inverse:
        return (real_cos - imag_sin, imag_cos + real_sin)
    return (real_cos + imag_sin, imag_cos - real_sin)


def inverse_symbol(wave_x, wave_y, wave_z, size_x, size_y, size_z):
    along_x = 2.0 * jnp.cos(wave_x.astype(jnp.float32) * (2.0 * jnp.pi / size_x)) - 2.0
    along_y = 2.0 * jnp.cos(wave_y.astype(jnp.float32) * (2.0 * jnp.pi / size_y)) - 2.0
    along_z = 2.0 * jnp.cos(wave_z.astype(jnp.float32) * (2.0 * jnp.pi / size_z)) - 2.0
    symbol = along_x[:, None, None] + along_y[None, :, None] + along_z[None, None, :]
    anchor = (
        (wave_x[:, None, None] == 0) & (wave_y[None, :, None] == 0) & (wave_z[None, None, :] == 0)
    )
    return jnp.where(anchor, 0.0, 1.0 / jnp.where(anchor, 1.0, symbol))


def solve_pressure(source):
    width_x, width_y, depth = source.shape
    across = lax.axis_size("gx")
    along = lax.axis_size("gy")
    full_x = width_x * across
    full_y = width_y * along
    cosine, sine = tables(depth)
    pair = (apply_table(source, cosine, 2), -apply_table(source, sine, 2))
    pair = in_one_piece((pair[0], pair[1]), "gx", 2, 0, 1)
    pair = transform(pair, 0, full_x, False)
    pair = in_one_piece((pair[0], pair[1]), "gy", 0, 1, 2)
    pair = transform(pair, 1, full_y, False)
    piece_x = full_x // along
    piece_z = depth // across
    wave_x = lax.axis_index("gy") * piece_x + jnp.arange(piece_x, dtype=jnp.int32)
    wave_y = jnp.arange(full_y, dtype=jnp.int32)
    wave_z = lax.axis_index("gx") * piece_z + jnp.arange(piece_z, dtype=jnp.int32)
    symbol = inverse_symbol(wave_x, wave_y, wave_z, full_x, full_y, depth)
    pair = (pair[0] * symbol, pair[1] * symbol)
    pair = transform(pair, 1, full_y, True)
    pair = in_one_piece((pair[0], pair[1]), "gy", 1, 0, 2)
    pair = transform(pair, 0, full_x, True)
    pair = in_one_piece((pair[0], pair[1]), "gx", 0, 2, 1)
    real_part = apply_table(pair[0], cosine, 2) - apply_table(pair[1], sine, 2)
    return real_part / (full_x * full_y * depth)


def per_device(
    species,
    diffusivity,
    lewis_number,
    velocity,
    layer_one,
    layer_two,
    layer_three,
    layer_four,
    heat_release,
    react_index,
    react_count,
):
    kinds = species.shape[0]
    fields = species
    for substep in range(SUBSTEPS):
        padded, kappa_pad = (
            extended(fields, (("gx", 1), ("gy", 2)), 1),
            extended(diffusivity[None], (("gx", 1), ("gy", 2)), 1),
        )
        coeffs = kappa_pad / lewis_number[:, None, None, None]
        fields, unused = diffuse(padded, coeffs)
    cells = fields.shape[1] * fields.shape[2] * fields.shape[3]
    flat = fields.reshape(kinds, cells)
    index_list = react_index.reshape(-1)
    capacity = index_list.shape[0]
    slots = capacity // BLOCK
    count_here = react_count.reshape(())
    chosen = jnp.take(flat, index_list, axis=1).astype(jnp.bfloat16)
    blocks = chosen.reshape(kinds, slots, BLOCK).transpose(1, 0, 2)
    rate_blocks = network(blocks, layer_one, layer_two, layer_three, layer_four).astype(jnp.float32)
    rate_rows = rate_blocks.transpose(1, 0, 2).reshape(kinds, capacity)
    live_mask = jnp.arange(capacity, dtype=jnp.int32) < count_here
    update = jnp.where(live_mask[None, :], react_step * rate_rows, 0.0)
    species_out = flat.at[:, index_list].add(update).reshape(fields.shape)
    heat_rows = jnp.where(
        live_mask, jnp.dot(heat_release, rate_rows, precision=lax.Precision.HIGHEST), 0.0
    )
    heat_field = (
        jnp.zeros((cells,), jnp.float32).at[index_list].add(heat_rows).reshape(fields.shape[1:])
    )
    flow_x = velocity[0]
    flow_y = velocity[1]
    flow_z = velocity[2]
    east_plane = from_behind(flow_x[0:1], "gx", -1)
    north_plane = from_behind(flow_y[:, 0:1], "gy", -1)
    divergence = (
        jnp.concatenate([flow_x[1:], east_plane], axis=0)
        - flow_x
        + (jnp.concatenate([flow_y[:, 1:], north_plane], axis=1) - flow_y)
        + (jnp.roll(flow_z, -1, 2) - flow_z)
    )
    source = divergence - heat_field
    pressure = solve_pressure(source)
    west_plane = from_behind(pressure[-1:], "gx", 1)
    south_plane = from_behind(pressure[:, -1:], "gy", 1)
    slope_x = pressure - jnp.concatenate([west_plane, pressure[:-1]], axis=0)
    slope_y = pressure - jnp.concatenate([south_plane, pressure[:, :-1]], axis=1)
    slope_z = pressure - jnp.roll(pressure, 1, 2)
    velocity_out = velocity - jnp.stack([slope_x, slope_y, slope_z])
    return (species_out, velocity_out)


def solution(mesh):
    return jax.shard_map(
        per_device,
        mesh=mesh,
        in_specs=(
            P(None, "gx", "gy", None),
            P("gx", "gy", None),
            P(),
            P(None, "gx", "gy", None),
            P(),
            P(),
            P(),
            P(),
            P(),
            P("gx", "gy", None),
            P("gx", "gy"),
        ),
        out_specs=(P(None, "gx", "gy", None), P(None, "gx", "gy", None)),
        check_vma=False,
    )
```

profile of v0, /device:TPU:1, one launch (start us, length us, event | category | flops | bytes accessed | tf_op | source)
XLA Modules:
  0.0 337.3 jit_solution(12481703621238023862)
XLA Ops:
  2.3 3.0 collective-permute-start
  6.6 2.9 collective-permute-start.1
  14.3 6.6 %fusion.256 = (f32[24,16,16,1]{3,2,1,0:T(8,128)}, f32[24,16,16,1]{3,2,1,0:T(8,128)}) fusion(f32[24,16,16,128]{3,2,1,0:T(8,128)} %param.11), kind=kLoop, calls=%fused_computation.314 | loop fusion | bytes 98304 | tf_op jit(solution)/shard_map/jit(_roll_static)/slice | solution.py:60
  20.9 3.9 %fusion.257 = (f32[24,16,16,127]{3,2,1,0:T(8,128)}, f32[24,16,16,127]{3,2,1,0:T(8,128)}) fusion(f32[24,16,16,128]{3,2,1,0:T(8,128)S(1)} %copy-done.3), kind=kLoop, calls=%fused_computation.315 | loop fusion | bytes 12484608 | tf_op jit(solution)/shard_map/jit(_roll_static)/slice | solution.py:60
  32.8 4.2 %collective-permute-start.4 = (f32[24,1,16,128]{3,2,1,0:T(8,128)}, f32[24,1,16,128]{3,2,1,0:T(8,128)S(1)}, u32[]{:S(2)}, u32[]{:S(2)}) collective-permute-start(f32[24,1,16,128]{3,2,1,0:T(8,128)} %get-tuple-element.28), channel_id=1, source_target_pairs={{16,0},{32,16},{48,32},{64,48},{80,64},{96,80},{112,96},{0,112},{1... | collective-permute-start | bytes 589832 | tf_op jit(solution)/shard_map/ppermute | solution.py:36
  37.0 3.5 %collective-permute-start.6 = (f32[24,16,1,128]{3,1,2,0:T(8,128)}, f32[24,16,1,128]{3,1,2,0:T(8,128)S(1)}, u32[]{:S(2)}, u32[]{:S(2)}) collective-permute-start(f32[24,16,1,128]{3,1,2,0:T(8,128)} %bitcast.258), channel_id=1, source_target_pairs={{1,0},{2,1},{3,2},{4,3},{5,4},{6,5},{7,6},{8,7},{9,8},{10,9},{11,1... | collective-permute-start | bytes 589832 | tf_op jit(solution)/shard_map/ppermute | solution.py:36
  43.5 3.8 %fusion.250 = (f32[24,16,16,127]{3,2,1,0:T(8,128)}, f32[24,16,16,127]{3,2,1,0:T(8,128)}) fusion(f32[24,18,18,128]{3,2,1,0:T(8,128)S(1)} %broadcast_divide_fusion), kind=kLoop, calls=%fused_computation.308 | loop fusion | bytes 12484608 | tf_op jit(solution)/shard_map/jit(_roll_static)/slice | solution.py:59
  47.2 3.7 %fusion.251 = (f32[24,16,16,1]{3,2,1,0:T(8,128)}, f32[24,16,16,1]{3,2,1,0:T(8,128)}) fusion(f32[24,18,18,128]{3,2,1,0:T(8,128)S(1)} %broadcast_divide_fusion), kind=kLoop, calls=%fused_computation.309 | loop fusion | bytes 98304 | tf_op jit(solution)/shard_map/jit(_roll_static)/slice | solution.py:59
  54.4 17.0 %fusion.38 = f32[24,16,16,128]{3,2,1,0:T(8,128)} fusion(f32[24,16,16,128]{3,2,1,0:T(8,128)} %param.11, f32[24,18,16,128]{3,2,1,0:T(8,128)} %constant_dynamic-update-slice_fusion, f32[24,16,1,128]{3,2,1,0:T(1,128)S(1)} %bitcast.254, f32[24,16,1,128]{3,2,1,0:T(1,128)S(1)} %bitcast.253, f32[24,1,16,128]{3,2,1,0:T(8,128)S(1)} %collective-permute-done.5, ...), kind=kLoop, calls=%fused_computation.54 | loop fusion | flops 35389440 | bytes 38928384 | tf_op jit(solution)/shard_map/add | solution.py:61
  71.4 6.6 %fusion.252 = (f32[24,16,16,1]{3,2,1,0:T(8,128)}, f32[24,16,16,1]{3,2,1,0:T(8,128)}) fusion(f32[24,16,16,128]{3,2,1,0:T(8,128)} %fusion.38), kind=kLoop, calls=%fused_computation.310 | loop fusion | bytes 98304 | tf_op jit(solution)/shard_map/jit(_roll_static)/slice | solution.py:60
  78.4 3.8 %collective-permute-start.10 = (f32[24,16,1,128]{3,1,2,0:T(8,128)S(1)}, f32[24,16,1,128]{3,1,2,0:T(8,128)S(1)}, u32[]{:S(2)}, u32[]{:S(2)}) collective-permute-start(f32[24,16,1,128]{3,1,2,0:T(8,128)S(1)} %bitcast.260), channel_id=1, source_target_pairs={{1,0},{2,1},{3,2},{4,3},{5,4},{6,5},{7,6},{8,7},{9,8},{10,9},{11,1... | collective-permute-start | bytes 589832 | tf_op jit(solution)/shard_map/ppermute | solution.py:36
  85.2 3.9 %fusion.253 = (f32[24,16,16,127]{3,2,1,0:T(8,128)}, f32[24,16,16,127]{3,2,1,0:T(8,128)}) fusion(f32[24,16,16,128]{3,2,1,0:T(8,128)S(1)} %copy-done.2), kind=kLoop, calls=%fused_computation.311 | loop fusion | bytes 12484608 | tf_op jit(solution)/shard_map/jit(_roll_static)/slice | solution.py:60
  89.1 3.0 collective-permute-start.12
  93.9 19.2 %fusion.23 = f32[24,16,16,128]{3,2,1,0:T(8,128)} fusion(f32[24,16,16,128]{3,2,1,0:T(8,128)} %fusion.38, f32[24,16,1,128]{3,2,1,0:T(1,128)S(1)} %bitcast.256, f32[24,1,16,128]{3,2,1,0:T(8,128)S(1)} %collective-permute-done.8, f32[24,1,16,128]{3,2,1,0:T(8,128)S(1)} %collective-permute-done.9, f32[24,16,1,128]{3,2,1,0:T(1,128)S(1)} %bitcast.255, ...), kind=kLoop, calls=%fused_computation.31 | loop fusion | flops 38535168 | bytes 35389440 | tf_op jit(solution)/shard_map/add | solution.py:61
  113.0 10.2 %copy.94 = f32[24,16,16,128]{0,3,2,1:T(8,128)} copy(f32[24,16,16,128]{3,2,1,0:T(8,128)} %fusion.23) | data formatting | bytes 6291456 | tf_op jit(solution)/shard_map/add | solution.py:61
  123.2 20.1 %gather_fusion = bf16[4096,24]{1,0:T(8,128)(2,1)} fusion(f32[24,32768]{0,1:T(8,128)} %bitcast.227, s32[4096]{0:T(1024)S(1)} %broadcast_clamp_fusion), kind=kCustom, calls=%fused_computation | custom fusion | bytes 409600 | tf_op jit(solution)/shard_map/jit(_take)/gather | solution.py:172
  144.9 21.6 %fusion.7 = bf16[32,800,128]{2,1,0:T(8,128)(2,1)} fusion(bf16[800,1600]{1,0:T(8,128)(2,1)S(1)} %copy-done, bf16[24,32,128]{2,0,1:T(8,128)(2,1)S(1)} %copy.95, pred[32,128]{1,0:T(8,128)(4,1)} %compare_and_fusion, bf16[1600,24]{0,1:T(8,128)(2,1)} %param.15), kind=kOutput, calls=%fused_computation.14 | convolution fusion | flops 10849583104 | bytes 9391104 | tf_op jit(solution)/shard_map/gf,bfr->bgr/dot_general | solution.py:72
  166.5 7.1 %fusion.59 = bf16[32,128,24]{1,2,0:T(8,128)(2,1)S(1)} fusion(bf16[32,800,128]{2,1,0:T(8,128)(2,1)} %fusion.7, bf16[400,800]{1,0:T(8,128)(2,1)} %param.17, bf16[24,400]{1,0:T(8,128)(2,1)} %param.18), kind=kOutput, calls=%fused_computation.93 | convolution fusion | flops 2708373504 | bytes 7409408 | tf_op jit(solution)/shard_map/sh,bhr->bsr/dot_general | solution.py:77
  173.8 22.3 %scatter_custom_fusion.1 = f32[32768]{0:T(1024)S(1)} fusion(s32[4096]{0:T(1024)S(1)} %bitcast.262, f32[4096]{0:T(1024)S(1)} %broadcast_select_fusion, f32[]{:T(128)} %constant.54.clone.1), kind=kCustom, calls=%fused_computation.189 | custom fusion | flops 4096 | bytes 131076 | tf_op jit(solution)/shard_map/scatter-add | solution.py:183
  199.8 4.8 %all-to-all-start = ((f32[8,1,8192]{2,1,0:T(1,128)}), f32[8,1,8192]{2,1,0:T(1,128)S(1)}, u32[]{:S(2)}, u32[]{:S(2)}) async-start(f32[8,1,8192]{2,1,0:T(1,128)} %reshape.236), calls=%async_computation | async-start | bytes 524288 | tf_op jit(solution)/shard_map/all_to_all | solution.py:17
  204.7 7.3 %all-to-all-done = f32[8,1,8192]{2,1,0:T(1,128)S(1)} async-done(((f32[8,1,8192]{2,1,0:T(1,128)}), f32[8,1,8192]{2,1,0:T(1,128)S(1)}, u32[]{:S(2)}, u32[]{:S(2)}) %all-to-all-start) | async-done | bytes 262176 | tf_op jit(solution)/shard_map/all_to_all | solution.py:17
  221.9 5.7 %all-to-all-start.1 = ((f32[16,1,4096]{2,1,0:T(1,128)}), f32[16,1,4096]{2,1,0:T(1,128)S(1)}, u32[]{:S(2)}, u32[]{:S(2)}) async-start(f32[16,1,4096]{2,1,0:T(1,128)} %reshape.238), calls=%async_computation.1 | async-start | bytes 524288 | tf_op jit(solution)/shard_map/all_to_all | solution.py:17
  227.7 7.0 %all-to-all-done.1 = f32[16,1,4096]{2,1,0:T(1,128)S(1)} async-done(((f32[16,1,4096]{2,1,0:T(1,128)}), f32[16,1,4096]{2,1,0:T(1,128)S(1)}, u32[]{:S(2)}, u32[]{:S(2)}) %all-to-all-start.1) | async-done | bytes 262176 | tf_op jit(solution)/shard_map/all_to_all | solution.py:17
  236.4 2.4 fusion.75
  238.8 2.6 fusion.73
  241.3 2.6 fusion.68
  245.2 2.4 fusion.66
  252.4 10.6 %all_to_all.72 = f32[16,1,4096]{2,1,0:T(1,128)S(1)} all-to-all(f32[16,1,4096]{2,1,0:T(1,128)S(1)} %reshape.240), channel_id=1, replica_groups=mesh['gx'=8,'gy'=16] {'gy'}, dimensions={0} | all-to-all | bytes 524288 | tf_op jit(solution)/shard_map/all_to_all | solution.py:17
  272.1 3.7 %all-to-all-start.3 = ((f32[8,1,8192]{2,1,0:T(1,128)}), f32[8,1,8192]{2,1,0:T(1,128)S(1)}, u32[]{:S(2)}, u32[]{:S(2)}) async-start(f32[8,1,8192]{2,1,0:T(1,128)} %reshape.242), calls=%async_computation.3 | async-start | bytes 524288 | tf_op jit(solution)/shard_map/all_to_all | solution.py:17
  275.8 7.4 %all-to-all-done.3 = f32[8,1,8192]{2,1,0:T(1,128)S(1)} async-done(((f32[8,1,8192]{2,1,0:T(1,128)}), f32[8,1,8192]{2,1,0:T(1,128)S(1)}, u32[]{:S(2)}, u32[]{:S(2)}) %all-to-all-start.3) | async-done | bytes 262176 | tf_op jit(solution)/shard_map/all_to_all | solution.py:17
  292.9 31.7 %scatter_fusion = f32[24,32768]{0,1:T(8,128)} fusion(f32[24,32768]{0,1:T(8,128)} %bitcast.228, s32[4096]{0:T(1024)S(1)} %bitcast.263, f32[4096,24]{1,0:T(8,128)S(1)} %copy.97), kind=kCustom, calls=%fused_computation.1 | custom fusion | flops 98304 | bytes 1196032 | tf_op jit(solution)/shard_map/scatter-add | solution.py:178
  324.6 11.5 %copy.117 = f32[24,16,16,128]{3,2,1,0:T(8,128)} copy(f32[24,16,16,128]{0,3,2,1:T(8,128)} %bitcast.229) | data formatting | bytes 6291456
  (148 shorter events, 69.2 us)
Async XLA Ops:
  0.6 144.3 %copy-start = (bf16[800,1600]{1,0:T(8,128)(2,1)S(1)}, bf16[800,1600]{1,0:T(8,128)(2,1)}, u32[]{:S(2)}) copy-start(bf16[800,1600]{1,0:T(8,128)(2,1)} %param.16) | copy-start | bytes 7680004
  2.3 30.5 %collective-permute-start = (f32[1,16,1,128]{3,2,1,0:T(1,128)}, f32[1,16,1,128]{3,2,1,0:T(1,128)S(1)}, u32[]{:S(2)}, u32[]{:S(2)}) collective-permute-start(f32[1,16,1,128]{3,2,1,0:T(1,128)} %get-tuple-element.41), channel_id=1, source_target_pairs={{0,1},{1,2},{2,3},{3,4},{4,5},{5,6},{6,7},{7,8},{8,9},{9,10},{10,1... | collective-permute-start | bytes 24584 | tf_op jit(solution)/shard_map/ppermute | solution.py:35
  6.6 30.4 %collective-permute-start.1 = (f32[1,1,16,128]{3,2,1,0:T(8,128)}, f32[1,1,16,128]{3,2,1,0:T(8,128)}, u32[]{:S(2)}, u32[]{:S(2)}) collective-permute-start(f32[1,1,16,128]{3,2,1,0:T(8,128)} %get-tuple-element.39), channel_id=1, source_target_pairs={{0,16},{16,32},{32,48},{48,64},{64,80},{80,96},{96,112},{112,0},{1... | collective-permute-start | bytes 24584 | tf_op jit(solution)/shard_map/ppermute | solution.py:35
  9.5 30.9 %collective-permute-start.2 = (f32[1,1,16,128]{3,2,1,0:T(8,128)}, f32[1,1,16,128]{3,2,1,0:T(8,128)}, u32[]{:S(2)}, u32[]{:S(2)}) collective-permute-start(f32[1,1,16,128]{3,2,1,0:T(8,128)} %get-tuple-element.40), channel_id=1, source_target_pairs={{16,0},{32,16},{48,32},{64,48},{80,64},{96,80},{112,96},{0,112},{1... | collective-permute-start | bytes 24584 | tf_op jit(solution)/shard_map/ppermute | solution.py:36
  11.7 28.8 %collective-permute-start.3 = (f32[1,16,1,128]{3,2,1,0:T(1,128)}, f32[1,16,1,128]{3,2,1,0:T(1,128)}, u32[]{:S(2)}, u32[]{:S(2)}) collective-permute-start(f32[1,16,1,128]{3,2,1,0:T(1,128)} %get-tuple-element.42), channel_id=1, source_target_pairs={{1,0},{2,1},{3,2},{4,3},{5,4},{6,5},{7,6},{8,7},{9,8},{10,9},{11,1... | collective-permute-start | bytes 24584 | tf_op jit(solution)/shard_map/ppermute | solution.py:36
  13.5 7.4 %copy-start.3 = (f32[24,16,16,128]{3,2,1,0:T(8,128)S(1)}, f32[24,16,16,128]{3,2,1,0:T(8,128)}, u32[]{:S(2)}) copy-start(f32[24,16,16,128]{3,2,1,0:T(8,128)} %param.11) | copy-start | bytes 9437188
  13.5 37.4 %collective-permute-start.5 = (f32[24,1,16,128]{3,2,1,0:T(8,128)}, f32[24,1,16,128]{3,2,1,0:T(8,128)S(1)}, u32[]{:S(2)}, u32[]{:S(2)}) collective-permute-start(f32[24,1,16,128]{3,2,1,0:T(8,128)} %get-tuple-element.29), channel_id=1, source_target_pairs={{0,16},{16,32},{32,48},{48,64},{64,80},{80,96},{96,112},{112,0},{1... | collective-permute-start | bytes 589832 | tf_op jit(solution)/shard_map/ppermute | solution.py:35
  20.9 7.9 %copy-start.8 = (s32[1,1,4096]{2,1,0:T(1,128)S(1)}, s32[1,1,4096]{2,1,0:T(1,128)}, u32[]{:S(2)}) copy-start(s32[1,1,4096]{2,1,0:T(1,128)} %param.20) | copy-start | bytes 49156
  32.7 7.7 %copy-start.9 = (f32[1,16,1,128]{3,2,1,0:T(1,128)}, f32[1,16,1,128]{3,2,1,0:T(1,128)S(1)}, u32[]{:S(2)}) copy-start(f32[1,16,1,128]{3,2,1,0:T(1,128)S(1)} %collective-permute-done) | copy-start | bytes 24580
  32.8 21.0 %collective-permute-start.4 = (f32[24,1,16,128]{3,2,1,0:T(8,128)}, f32[24,1,16,128]{3,2,1,0:T(8,128)S(1)}, u32[]{:S(2)}, u32[]{:S(2)}) collective-permute-start(f32[24,1,16,128]{3,2,1,0:T(8,128)} %get-tuple-element.28), channel_id=1, source_target_pairs={{16,0},{32,16},{48,32},{64,48},{80,64},{96,80},{112,96},{0,112},{1... | collective-permute-start | bytes 589832 | tf_op jit(solution)/shard_map/ppermute | solution.py:36
  37.0 17.5 %collective-permute-start.6 = (f32[24,16,1,128]{3,1,2,0:T(8,128)}, f32[24,16,1,128]{3,1,2,0:T(8,128)S(1)}, u32[]{:S(2)}, u32[]{:S(2)}) collective-permute-start(f32[24,16,1,128]{3,1,2,0:T(8,128)} %bitcast.258), channel_id=1, source_target_pairs={{1,0},{2,1},{3,2},{4,3},{5,4},{6,5},{7,6},{8,7},{9,8},{10,9},{11,1... | collective-permute-start | bytes 589832 | tf_op jit(solution)/shard_map/ppermute | solution.py:36
  40.5 14.0 %collective-permute-start.7 = (f32[24,16,1,128]{3,1,2,0:T(8,128)}, f32[24,16,1,128]{3,1,2,0:T(8,128)S(1)}, u32[]{:S(2)}, u32[]{:S(2)}) collective-permute-start(f32[24,16,1,128]{3,1,2,0:T(8,128)} %bitcast.257), channel_id=1, source_target_pairs={{0,1},{1,2},{2,3},{3,4},{4,5},{5,6},{6,7},{7,8},{8,9},{9,10},{10,1... | collective-permute-start | bytes 589832 | tf_op jit(solution)/shard_map/ppermute | solution.py:35
  40.5 155.7 %collective-permute-start.13 = (f32[16,1,128]{2,1,0:T(1,128)}, f32[16,1,128]{2,1,0:T(1,128)S(1)}, u32[]{:S(2)}, u32[]{:S(2)}) collective-permute-start(f32[16,1,128]{2,1,0:T(1,128)} %slice.307), channel_id=1, source_target_pairs={{0,15},{1,0},{2,1},{3,2},{4,3},{5,4},{6,5},{7,6},{8,7},{9,8},{10,9... | collective-permute-start | bytes 24584 | tf_op jit(solution)/shard_map/ppermute | solution.py:49
  71.4 6.6 %copy-start.2 = (f32[24,16,16,128]{3,2,1,0:T(8,128)S(1)}, f32[24,16,16,128]{3,2,1,0:T(8,128)}, u32[]{:S(2)}) copy-start(f32[24,16,16,128]{3,2,1,0:T(8,128)} %fusion.38) | copy-start | bytes 9437188
  78.4 10.7 %collective-permute-start.10 = (f32[24,16,1,128]{3,1,2,0:T(8,128)S(1)}, f32[24,16,1,128]{3,1,2,0:T(8,128)S(1)}, u32[]{:S(2)}, u32[]{:S(2)}) collective-permute-start(f32[24,16,1,128]{3,1,2,0:T(8,128)S(1)} %bitcast.260), channel_id=1, source_target_pairs={{1,0},{2,1},{3,2},{4,3},{5,4},{6,5},{7,6},{8,7},{9,8},{10,9},{11,1... | collective-permute-start | bytes 589832 | tf_op jit(solution)/shard_map/ppermute | solution.py:36
  82.2 9.9 %collective-permute-start.11 = (f32[24,16,1,128]{3,1,2,0:T(8,128)S(1)}, f32[24,16,1,128]{3,1,2,0:T(8,128)S(1)}, u32[]{:S(2)}, u32[]{:S(2)}) collective-permute-start(f32[24,16,1,128]{3,1,2,0:T(8,128)S(1)} %bitcast.259), channel_id=1, source_target_pairs={{0,1},{1,2},{2,3},{3,4},{4,5},{5,6},{6,7},{7,8},{8,9},{9,10},{10,1... | collective-permute-start | bytes 589832 | tf_op jit(solution)/shard_map/ppermute | solution.py:35
  82.2 11.7 %collective-permute-start.8 = (f32[24,1,16,128]{3,2,1,0:T(8,128)S(1)}, f32[24,1,16,128]{3,2,1,0:T(8,128)S(1)}, u32[]{:S(2)}, u32[]{:S(2)}) collective-permute-start(f32[24,1,16,128]{3,2,1,0:T(8,128)S(1)} %get-tuple-element.21), channel_id=1, source_target_pairs={{16,0},{32,16},{48,32},{64,48},{80,64},{96,80},{112,96},{0,112},{1... | collective-permute-start | bytes 589832 | tf_op jit(solution)/shard_map/ppermute | solution.py:36
  82.9 11.0 %collective-permute-start.9 = (f32[24,1,16,128]{3,2,1,0:T(8,128)S(1)}, f32[24,1,16,128]{3,2,1,0:T(8,128)S(1)}, u32[]{:S(2)}, u32[]{:S(2)}) collective-permute-start(f32[24,1,16,128]{3,2,1,0:T(8,128)S(1)} %get-tuple-element.20), channel_id=1, source_target_pairs={{0,16},{16,32},{32,48},{48,64},{64,80},{80,96},{96,112},{112,0},{1... | collective-permute-start | bytes 589832 | tf_op jit(solution)/shard_map/ppermute | solution.py:35
  89.1 107.1 %collective-permute-start.12 = (f32[1,16,128]{2,1,0:T(8,128)}, f32[1,16,128]{2,1,0:T(8,128)}, u32[]{:S(2)}, u32[]{:S(2)}) collective-permute-start(f32[1,16,128]{2,1,0:T(8,128)} %slice_bitcast_fusion.3), channel_id=1, source_target_pairs={{0,112},{16,0},{32,16},{48,32},{64,48},{80,64},{96,80},{112,96},{1... | collective-permute-start | bytes 24584 | tf_op jit(solution)/shard_map/ppermute | solution.py:49
  166.5 7.1 %copy-start.11 = (f32[24]{0:T(128)S(1)}, f32[24]{0:T(128)}, u32[]{:S(2)}) copy-start(f32[24]{0:T(128)} %param.19) | copy-start | bytes 292
  166.5 29.7 %copy-start.6 = (f32[16,15,128]{2,1,0:T(8,128)S(1)}, f32[16,15,128]{2,1,0:T(8,128)}, u32[]{:S(2)}) copy-start(f32[16,15,128]{2,1,0:T(8,128)} %slice.306) | copy-start | bytes 368644
  166.5 29.7 %copy-start.7 = (f32[15,16,128]{2,1,0:T(8,128)S(1)}, f32[15,16,128]{2,1,0:T(8,128)}, u32[]{:S(2)}) copy-start(f32[15,16,128]{2,1,0:T(8,128)} %slice_bitcast_fusion.2) | copy-start | bytes 368644
  173.6 31.0 %copy-start.13 = (pred[8]{0:T(512)(128)(4,1)S(1)}, pred[8]{0:T(512)(128)(4,1)}, u32[]{:S(2)}) copy-start(pred[8]{0:T(512)(128)(4,1)} %fusion.165) | copy-start | bytes 28
  173.6 31.0 %copy-start.14 = (pred[256]{0:T(512)(128)(4,1)S(1)}, pred[256]{0:T(512)(128)(4,1)}, u32[]{:S(2)}) copy-start(pred[256]{0:T(512)(128)(4,1)} %iota_compare_fusion.3) | copy-start | bytes 772
  199.8 12.3 %all-to-all-start = ((f32[8,1,8192]{2,1,0:T(1,128)}), f32[8,1,8192]{2,1,0:T(1,128)S(1)}, u32[]{:S(2)}, u32[]{:S(2)}) async-start(f32[8,1,8192]{2,1,0:T(1,128)} %reshape.236), calls=%async_computation | async-start | bytes 524288 | tf_op jit(solution)/shard_map/all_to_all | solution.py:17
  218.6 9.0 %copy-start.10 = (f32[256]{0:T(256)S(1)}, f32[256]{0:T(256)}, u32[]{:S(2)}) copy-start(f32[256]{0:T(256)} %multiply_add_fusion) | copy-start | bytes 3076
  218.6 9.0 %copy-start.12 = (f32[8]{0:T(128)S(1)}, f32[8]{0:T(128)}, u32[]{:S(2)}) copy-start(f32[8]{0:T(128)} %multiply_add_fusion.2) | copy-start | bytes 100
  221.9 12.8 %all-to-all-start.1 = ((f32[16,1,4096]{2,1,0:T(1,128)}), f32[16,1,4096]{2,1,0:T(1,128)S(1)}, u32[]{:S(2)}, u32[]{:S(2)}) async-start(f32[16,1,4096]{2,1,0:T(1,128)} %reshape.238), calls=%async_computation.1 | async-start | bytes 524288 | tf_op jit(solution)/shard_map/all_to_all | solution.py:17
  272.1 11.1 %all-to-all-start.3 = ((f32[8,1,8192]{2,1,0:T(1,128)}), f32[8,1,8192]{2,1,0:T(1,128)S(1)}, u32[]{:S(2)}, u32[]{:S(2)}) async-start(f32[8,1,8192]{2,1,0:T(1,128)} %reshape.242), calls=%async_computation.3 | async-start | bytes 524288 | tf_op jit(solution)/shard_map/all_to_all | solution.py:17
  288.9 47.2 %collective-permute-start.14 = (f32[1,16,128]{2,1,0:T(8,128)S(1)}, f32[1,16,128]{2,1,0:T(8,128)S(1)}, u32[]{:S(2)}, u32[]{:S(2)}) collective-permute-start(f32[1,16,128]{2,1,0:T(8,128)S(1)} %slice.318), channel_id=1, source_target_pairs={{0,16},{16,32},{32,48},{48,64},{64,80},{80,96},{96,112},{112,0},{1... | collective-permute-start | bytes 24584 | tf_op jit(solution)/shard_map/ppermute | solution.py:49
  290.0 46.2 %collective-permute-start.15 = (f32[16,1,128]{2,1,0:T(1,128)S(1)}, f32[16,1,128]{2,1,0:T(1,128)S(1)}, u32[]{:S(2)}, u32[]{:S(2)}) collective-permute-start(f32[16,1,128]{2,1,0:T(1,128)S(1)} %slice.320), channel_id=1, source_target_pairs={{0,1},{1,2},{2,3},{3,4},{4,5},{5,6},{6,7},{7,8},{8,9},{9,10},{10,1... | collective-permute-start | bytes 24584 | tf_op jit(solution)/shard_map/ppermute | solution.py:49
  324.6 12.5 %copy-start.1 = (bf16[800,1600]{1,0:T(8,128)(2,1)S(1)}, bf16[800,1600]{1,0:T(8,128)(2,1)}, u32[]{:S(2)}) copy-start(bf16[800,1600]{1,0:T(8,128)(2,1)} %param.16) | copy-start | bytes 7680004
  (2 other events, 9.4 us)
where the time goes:
time: 343 us; the launch traced here: 337 us
  other arithmetic  103 us (30%)
  local copies, waits for them, and re-layouts  100 us (29%)
  matrix products  53 us (15%)
  starting transfers between devices  44.8 us (13%)
  waiting for transfers between devices  23.6 us (7%)
  blocking collectives  10.6 us (3%)
    add x2, other arithmetic, diffuse(): center + diffuse_step * (east_flux - west_flux + (north_flux - south_flux...  36.2 us
    scatter-add x1, other arithmetic, per_device(): species_out = flat.at[:, index_list].add(update).reshape(fields.shape)  31.7 us
    unnamed x45, local copies, waits for them, and re-layouts  23.6 us
    scatter-add x1, other arithmetic, per_device(): jnp.zeros((cells,), jnp.float32).at[index_list].add(heat_rows)  22.3 us
    all_to_all x3, waiting for transfers between devices, in_one_piece(): lax.all_to_all(both, axis, split_axis=split_dim, concat_axis=concat_dim,...  21.7 us
    gather x2, local copies, waits for them, and re-layouts, per_device(): chosen = jnp.take(flat, index_list, axis=1).astype(jnp.bfloat16)  21.7 us
    dot_general x1, matrix products, network(): jnp.einsum('gf,bfr->bgr', second, hidden, preferred_element_type=jnp.floa...  21.6 us
    slice x4, local copies, waits for them, and re-layouts, diffuse(): jnp.roll(center, 1, 3)  21 us
  transfers between devices with their start and end apart: 19, of which 4 were waited for; matrix products, arithmetic and copies ran while one was open for 62% of the time, Pallas kernels for 0%

commit v1 on v0

--- a/solution.py
+++ b/solution.py
@@ -1,7 +1,161 @@
+import functools
+import numpy as np
 import jax
 import jax.numpy as jnp
 from jax import lax
+from jax.experimental import pallas as pl
+from jax.experimental.pallas import tpu as pltpu
+
 from jax.sharding import PartitionSpec as P
+
+MESH = pl.DeviceIdType.MESH
+HI = lax.Precision.HIGHEST
+
+
+def real_basis(n):
+    k = np.arange(n)
+    j = np.arange(n)
+    wave = np.where(k <= n // 2, k, k - n // 2)
+    ang = 2.0 * np.pi * ((wave[:, None] * j[None, :]) % n) / n
+    rows = np.where((k <= n // 2)[:, None], np.cos(ang), np.sin(ang)) * np.sqrt(2.0 / n)
+    rows[0] *= np.sqrt(0.5)
+    rows[n // 2] *= np.sqrt(0.5)
+    lam = 2.0 * np.cos(2.0 * np.pi * wave / n) - 2.0
+    return rows.astype(np.float32), lam.astype(np.float32)
+
+
+def mm(a, b, dims, precision=HI):
+    return lax.dot_general(a, b, (dims, ((), ())), precision=precision, preferred_element_type=jnp.float32)
+
+
+def units(grid, lane):
+    turned = []
+    for d in range(8):
+        w = grid[d]
+        for u in range(1, 8):
+            w = jnp.where(lane == u, grid[(u + d) % 8], w)
+        turned.append(w if d == 0 else pltpu.roll(w, d * 16, 1))
+    out = []
+    for v in range(8):
+        acc = turned[(0 - v) % 8]
+        for u in range(1, 8):
+            acc = jnp.where(lane == u, turned[(u - v) % 8], acc)
+        out.append(acc)
+    return out
+
+
+def poisson_kernel(gx_n, gy_n, src, vel, fz, fx, fxt, fy, lamx, lamy, lamz, out,
+                   sbuf, rbuf, tbuf, pbuf, send_sem, recv_sem, send_sem2, recv_sem2):
+    gx = lax.axis_index("gx")
+    gy = lax.axis_index("gy")
+    n = gx_n * gy_n
+    me = gx * gy_n + gy
+    barrier = pltpu.get_barrier_semaphore()
+
+    def greet(i, c):
+        t = lax.rem(me + i, n)
+        pl.semaphore_signal(barrier, inc=1, device_id=(t // gy_n, lax.rem(t, gy_n)), device_id_type=MESH)
+        return c
+    lax.fori_loop(1, n, greet, 0)
+    zt = mm(fz[...], src[...], ((1,), (1,)))
+    sbuf[:, 0, :] = zt[:, :128]
+    sbuf[:, 1, :] = zt[:, 128:]
+    pl.semaphore_wait(barrier, n - 1)
+
+    def send(i, c):
+        t = lax.rem(me + i, n)
+        ta, tb = t // gy_n, lax.rem(t, gy_n)
+        pltpu.make_async_remote_copy(
+            src_ref=sbuf.at[t], dst_ref=rbuf.at[gy, gx], send_sem=send_sem, recv_sem=recv_sem,
+            device_id=(ta, tb), device_id_type=MESH).start()
+        return c
+    lax.fori_loop(1, n, send, 0)
+    own = pltpu.make_async_copy(sbuf.at[me], rbuf.at[gy, gx], recv_sem)
+    own.start()
+    lane = lax.broadcasted_iota(jnp.int32, (8, 128), 1) // 16
+    col = lax.broadcasted_iota(jnp.int32, (8, 128), 1)
+    mode = lax.broadcasted_iota(jnp.int32, (1, 128), 1)
+    lz = jnp.sum(jnp.where(mode == me, lamz[...], 0.0), axis=1, keepdims=True)
+    sym = lamx[...] + lamy[...] + lz
+    anchor = (lax.broadcasted_iota(jnp.int32, (128, 256), 0) == 0) & (lax.broadcasted_iota(jnp.int32, (128, 256), 1) == 0) & (me == 0)
+    g = jnp.where(anchor, 0.0, 1.0 / jnp.where(anchor, 1.0, sym))
+    pltpu.make_async_copy(rbuf, rbuf, recv_sem).wait()
+    pltpu.make_async_copy(sbuf.at[pl.ds(0, n - 1)], sbuf.at[pl.ds(0, n - 1)], send_sem).wait()
+
+    planes = [[None, None] for _ in range(16)]
+    for h in range(2):
+        for bh in range(2):
+            got = units([rbuf[bh * 8 + b, :, h, :] for b in range(8)], lane)
+            for xlo in range(8):
+                planes[h * 8 + xlo][bh] = got[xlo]
+    plane = jnp.concatenate([jnp.concatenate(p, axis=1) for p in planes], axis=0)
+    t = mm(fx[...], plane, ((1,), (0,)))
+    t = mm(t, fy[...], ((1,), (1,))) * g
+    t = mm(t, fy[...], ((1,), (0,)))
+    p = mm(fxt[...], t, ((1,), (0,)))
+    px = [[p[x * 8:(x + 1) * 8, bh * 128:(bh + 1) * 128] for bh in range(2)] for x in range(16)]
+    before = pltpu.roll(p, 1, 1)
+    for bh in range(2):
+        edge_x = pltpu.roll(px[15][bh], 1, 0)
+        edge_y = before[0:8, bh * 128:(bh + 1) * 128]
+        for x in range(1, 16):
+            edge_y = jnp.where(col % 16 == x, pltpu.roll(before[x * 8:(x + 1) * 8, bh * 128:(bh + 1) * 128], x, 1), edge_y)
+        for h in range(2):
+            got = units([px[h * 8 + xlo][bh] for xlo in range(8)], lane)
+            for b in range(8):
+                tbuf[bh * 8 + b, :, h, :] = got[b]
+        for b in range(8):
+            ex = edge_x if b == 0 else pltpu.roll(edge_x, 128 - b * 16, 1)
+            ey = pltpu.roll(edge_y, (128 - b * 16 + 16) % 128, 1) if b != 1 else edge_y
+            tbuf[bh * 8 + b, :, 2, :] = jnp.where(lane == 0, ex, ey)
+
+    def back(i, c):
+        t = lax.rem(me + i, n)
+        ta, tb = t // gy_n, lax.rem(t, gy_n)
+        pltpu.make_async_remote_copy(
+            src_ref=tbuf.at[tb, ta], dst_ref=pbuf.at[me], send_sem=send_sem2, recv_sem=recv_sem2,
+            device_id=(ta, tb), device_id_type=MESH).start()
+        return c
+    lax.fori_loop(1, n, back, 0)
+    own = pltpu.make_async_copy(tbuf.at[gy, gx], pbuf.at[me], recv_sem2)
+    own.start()
+    pltpu.make_async_copy(pbuf, pbuf, recv_sem2).wait()
+    pltpu.make_async_copy(pbuf.at[pl.ds(0, n - 1)], pbuf.at[pl.ds(0, n - 1)], send_sem2).wait()
+    rows = [mm(pbuf[:, h, :], fz[...], ((0,), (0,))) for h in range(3)]
+    q = jnp.concatenate(rows[:2], axis=0)
+    west = rows[2][0:16]
+    south = rows[2][16:32]
+    out[2] = vel[2] - (q - pltpu.roll(q, 1, 1))
+    out[0] = vel[0] - (q - jnp.concatenate([west, q[:240]], axis=0))
+    sub = lax.broadcasted_iota(jnp.int32, (16, 128), 0)
+    for x in range(16):
+        cur = q[x * 16:(x + 1) * 16]
+        prev = jnp.where(sub == 0, jnp.broadcast_to(south[x:x + 1], (16, 128)), pltpu.roll(cur, 1, 0))
+        out[1, x * 16:(x + 1) * 16] = vel[1, x * 16:(x + 1) * 16] - (cur - prev)
+
+
+def poisson(source, velocity):
+    gx_n, gy_n = lax.axis_size("gx"), lax.axis_size("gy")
+    fz, lz = real_basis(128)
+    fx, lx = real_basis(128)
+    fy, ly = real_basis(256)
+    fxp = fx.reshape(128, 8, 16).transpose(0, 2, 1).reshape(128, 128)
+    vm = pl.BlockSpec(memory_space=pltpu.VMEM)
+    args = (source.reshape(256, 128), velocity.reshape(3, 256, 128), jnp.asarray(fz), jnp.asarray(fxp), jnp.asarray(np.ascontiguousarray(fxp.T)), jnp.asarray(fy),
+            jnp.asarray(lx[:, None]), jnp.asarray(ly[None, :]), jnp.asarray(lz[None, :]))
+    out = pl.pallas_call(
+        functools.partial(poisson_kernel, gx_n, gy_n),
+        out_shape=jax.ShapeDtypeStruct((3, 256, 128), jnp.float32),
+        in_specs=[vm] * len(args), out_specs=vm,
+        scratch_shapes=[
+            pltpu.VMEM((128, 2, 128), jnp.float32), pltpu.VMEM((16, 8, 2, 128), jnp.float32),
+            pltpu.VMEM((16, 8, 3, 128), jnp.float32), pltpu.VMEM((128, 3, 128), jnp.float32),
+            pltpu.SemaphoreType.DMA, pltpu.SemaphoreType.DMA, pltpu.SemaphoreType.DMA, pltpu.SemaphoreType.DMA],
+        compiler_params=pltpu.CompilerParams(collective_id=1, has_side_effects=True),
+        name="poisson",
+    )(*args)
+    return out.reshape(velocity.shape)
+
 
 SUBSTEPS = 2
 BLOCK = 128
@@ -77,68 +231,6 @@
     return jnp.einsum("sh,bhr->bsr", fourth, hidden, preferred_element_type=jnp.float32).astype(
         jnp.bfloat16
     )
-
-
-def tables(length):
-    counter = jnp.arange(length, dtype=jnp.int32)
-    phase = counter[:, None] * counter[None, :] % length
-    angle = phase.astype(jnp.float32) * (2.0 * jnp.pi / length)
-    return (jnp.cos(angle), jnp.sin(angle))
-
-
-def apply_table(values, matrix, axis):
-    product = jnp.tensordot(values, matrix, axes=([axis], [0]), precision=lax.Precision.HIGHEST)
-    return jnp.moveaxis(product, -1, axis)
-
-
-def transform(pair, axis, length, inverse):
-    cosine, sine = tables(length)
-    real_part, imag_part = pair
-    real_cos = apply_table(real_part, cosine, axis)
-    real_sin = apply_table(real_part, sine, axis)
-    imag_cos = apply_table(imag_part, cosine, axis)
-    imag_sin = apply_table(imag_part, sine, axis)
-    if inverse:
-        return (real_cos - imag_sin, imag_cos + real_sin)
-    return (real_cos + imag_sin, imag_cos - real_sin)
-
-
-def inverse_symbol(wave_x, wave_y, wave_z, size_x, size_y, size_z):
-    along_x = 2.0 * jnp.cos(wave_x.astype(jnp.float32) * (2.0 * jnp.pi / size_x)) - 2.0
-    along_y = 2.0 * jnp.cos(wave_y.astype(jnp.float32) * (2.0 * jnp.pi / size_y)) - 2.0
-    along_z = 2.0 * jnp.cos(wave_z.astype(jnp.float32) * (2.0 * jnp.pi / size_z)) - 2.0
-    symbol = along_x[:, None, None] + along_y[None, :, None] + along_z[None, None, :]
-    anchor = (
-        (wave_x[:, None, None] == 0) & (wave_y[None, :, None] == 0) & (wave_z[None, None, :] == 0)
-    )
-    return jnp.where(anchor, 0.0, 1.0 / jnp.where(anchor, 1.0, symbol))
-
-
-def solve_pressure(source):
-    width_x, width_y, depth = source.shape
-    across = lax.axis_size("gx")
-    along = lax.axis_size("gy")
-    full_x = width_x * across
-    full_y = width_y * along
-    cosine, sine = tables(depth)
-    pair = (apply_table(source, cosine, 2), -apply_table(source, sine, 2))
-    pair = in_one_piece((pair[0], pair[1]), "gx", 2, 0, 1)
-    pair = transform(pair, 0, full_x, False)
-    pair = in_one_piece((pair[0], pair[1]), "gy", 0, 1, 2)
-    pair = transform(pair, 1, full_y, False)
-    piece_x = full_x // along
-    piece_z = depth // across
-    wave_x = lax.axis_index("gy") * piece_x + jnp.arange(piece_x, dtype=jnp.int32)
-    wave_y = jnp.arange(full_y, dtype=jnp.int32)
-    wave_z = lax.axis_index("gx") * piece_z + jnp.arange(piece_z, dtype=jnp.int32)
-    symbol = inverse_symbol(wave_x, wave_y, wave_z, full_x, full_y, depth)
-    pair = (pair[0] * symbol, pair[1] * symbol)
-    pair = transform(pair, 1, full_y, True)
-    pair = in_one_piece((pair[0], pair[1]), "gy", 1, 0, 2)
-    pair = transform(pair, 0, full_x, True)
-    pair = in_one_piece((pair[0], pair[1]), "gx", 0, 2, 1)
-    real_part = apply_table(pair[0], cosine, 2) - apply_table(pair[1], sine, 2)
-    return real_part / (full_x * full_y * depth)
 
 
 def per_device(
@@ -194,13 +286,7 @@
         + (jnp.roll(flow_z, -1, 2) - flow_z)
     )
     source = divergence - heat_field
-    pressure = solve_pressure(source)
-    west_plane = from_behind(pressure[-1:], "gx", 1)
-    south_plane = from_behind(pressure[:, -1:], "gy", 1)
-    slope_x = pressure - jnp.concatenate([west_plane, pressure[:-1]], axis=0)
-    slope_y = pressure - jnp.concatenate([south_plane, pressure[:, :-1]], axis=1)
-    slope_z = pressure - jnp.roll(pressure, 1, 2)
-    velocity_out = velocity - jnp.stack([slope_x, slope_y, slope_z])
+    velocity_out = poisson(source, velocity)
     return (species_out, velocity_out)
 
 

time: 343 us -> 264 us (0.77); the launches traced: 337 us -> 263 us
  matrix products: 53 us -> 27.9 us
  Pallas kernels: 0 us -> 24.7 us
  starting transfers between devices: 44.8 us -> 26.3 us
  local copies, waits for them, and re-layouts: 100 us -> 82 us
  waiting for transfers between devices: 23.6 us -> 8.7 us
  other arithmetic: 103 us -> 92 us
  blocking collectives: 10.6 us -> 0 us
    pallas_call x0 -> x1, Pallas kernels: none -> 24.7 us  [poisson(): pl.pallas_call(functools.partial(poisson_kernel, gx_n, gy_n), out_shape=j...]
    all_to_all x3 -> x0, waiting for transfers between devices: 21.7 us -> none  [in_one_piece(): lax.all_to_all(both, axis, split_axis=split_dim, concat_axis=concat_dim,...]
    dot_general x12 -> x0, matrix products: 20 us -> none  [apply_table(): jnp.tensordot(values, matrix, axes=([axis], [0]), precision=lax.Precision...]
    all_to_all x3 -> x0, starting transfers between devices: 14.2 us -> none  [in_one_piece(): lax.all_to_all(both, axis, split_axis=split_dim, concat_axis=concat_dim,...]
    all_to_all x1 -> x0, blocking collectives: 10.6 us -> none  [in_one_piece(): lax.all_to_all(both, axis, split_axis=split_dim, concat_axis=concat_dim,...]
    unnamed x45 -> x26, local copies, waits for them, and re-layouts: 23.6 us -> 15.9 us
    ppermute x4 -> x2, starting transfers between devices: 7.24 us -> 1.44 us  [from_behind(): lax.ppermute(value, axis, [(i, (i + by) % peers) for i in range(peers)])]
    all_to_all x4 -> x0, other arithmetic: 5.17 us -> none  [in_one_piece(): lax.all_to_all(both, axis, split_axis=split_dim, concat_axis=concat_dim,...]
  transfers between devices with their start and end apart: 19 -> 14, of which waited for: 4 -> 3; matrix products, arithmetic and copies ran while one was open for 62% -> 11% of each run, Pallas kernels for 0% -> 0%
where the time goes in v1:
time: 264 us; the launch traced here: 263 us
  other arithmetic  92 us (35%)
  local copies, waits for them, and re-layouts  82 us (31%)
  matrix products  27.9 us (11%)
  starting transfers between devices  26.3 us (10%)
  Pallas kernels  24.7 us (9%)
  waiting for transfers between devices  8.7 us (3%)
    add x2, other arithmetic, diffuse(): center + diffuse_step * (east_flux - west_flux + (north_flux - south_flux...  36.1 us
    scatter-add x1, other arithmetic, per_device(): species_out = flat.at[:, index_list].add(update).reshape(fields.shape)  31.6 us
    pallas_call x1, Pallas kernels, poisson(): pl.pallas_call(functools.partial(poisson_kernel, gx_n, gy_n), out_shape=j...  24.7 us
    scatter-add x1, other arithmetic, per_device(): jnp.zeros((cells,), jnp.float32).at[index_list].add(heat_rows)  21.9 us
    gather x2, local copies, waits for them, and re-layouts, per_device(): chosen = jnp.take(flat, index_list, axis=1).astype(jnp.bfloat16)  21.7 us
    slice x4, local copies, waits for them, and re-layouts, diffuse(): jnp.roll(center, 1, 3)  20.9 us
    dot_general x1, matrix products, network(): jnp.einsum('gf,bfr->bgr', second, hidden, preferred_element_type=jnp.floa...  20.6 us
    ppermute x6, starting transfers between devices, extended(): lax.ppermute(leading, axis, [(b, a) for a, b in up])  17.8 us
  transfers between devices with their start and end apart: 14, of which 3 were waited for; matrix products, arithmetic and copies ran while one was open for 11% of the time, Pallas kernels for 0%

profile of v1, /device:TPU:1, one launch (start us, length us, event | category | flops | bytes accessed | tf_op | source)
XLA Modules:
  0.0 263.2 jit_solution(11390384924607320825)
XLA Ops:
  0.6 1.0 fusion.101
  1.7 3.1 %collective-permute-start = (f32[1,16,1,128]{3,2,1,0:T(1,128)S(1)}, f32[1,16,1,128]{3,2,1,0:T(1,128)S(1)}, u32[]{:S(2)}, u32[]{:S(2)}) collective-permute-start(f32[1,16,1,128]{3,2,1,0:T(1,128)S(1)} %get-tuple-element.37), channel_id=1, source_target_pairs={{0,1},{1,2},{2,3},{3,4},{4,5},{5,6},{6,7},{7,8},{8,9},{9,10},{10,1... | collective-permute-start | bytes 24584 | tf_op jit(solution)/shard_map/ppermute | solution.py:189
  5.5 2.9 %collective-permute-start.1 = (f32[1,1,16,128]{3,2,1,0:T(8,128)S(1)}, f32[1,1,16,128]{3,2,1,0:T(8,128)S(1)}, u32[]{:S(2)}, u32[]{:S(2)}) collective-permute-start(f32[1,1,16,128]{3,2,1,0:T(8,128)S(1)} %get-tuple-element.35), channel_id=1, source_target_pairs={{0,16},{16,32},{32,48},{48,64},{64,80},{80,96},{96,112},{112,0},{1... | collective-permute-start | bytes 24584 | tf_op jit(solution)/shard_map/ppermute | solution.py:189
  8.4 2.2 collective-permute-start.2
  10.6 1.1 fusion.98
  11.7 0.8 collective-permute-start.5
  12.5 6.6 %fusion.95 = (f32[24,16,16,1]{3,2,1,0:T(8,128)}, f32[24,16,16,1]{3,2,1,0:T(8,128)}) fusion(f32[24,16,16,128]{3,2,1,0:T(8,128)} %param.18), kind=kLoop, calls=%fused_computation.145 | loop fusion | bytes 98304 | tf_op jit(solution)/shard_map/jit(_roll_static)/slice | solution.py:214
  19.1 4.0 %fusion.96 = (f32[24,16,16,127]{3,2,1,0:T(8,128)}, f32[24,16,16,127]{3,2,1,0:T(8,128)}) fusion(f32[24,16,16,128]{3,2,1,0:T(8,128)S(1)} %copy-done.3), kind=kLoop, calls=%fused_computation.146 | loop fusion | bytes 12484608 | tf_op jit(solution)/shard_map/jit(_roll_static)/slice | solution.py:214
  25.1 4.3 %collective-permute-start.4 = (f32[24,1,16,128]{3,2,1,0:T(8,128)S(1)}, f32[24,1,16,128]{3,2,1,0:T(8,128)S(1)}, u32[]{:S(2)}, u32[]{:S(2)}) collective-permute-start(f32[24,1,16,128]{3,2,1,0:T(8,128)S(1)} %get-tuple-element.28), channel_id=1, source_target_pairs={{16,0},{32,16},{48,32},{64,48},{80,64},{96,80},{112,96},{0,112},{1... | collective-permute-start | bytes 589832 | tf_op jit(solution)/shard_map/ppermute | solution.py:190
  29.4 3.5 %collective-permute-start.6 = (f32[24,16,1,128]{3,1,2,0:T(8,128)S(1)}, f32[24,16,1,128]{3,1,2,0:T(8,128)S(1)}, u32[]{:S(2)}, u32[]{:S(2)}) collective-permute-start(f32[24,16,1,128]{3,1,2,0:T(8,128)S(1)} %bitcast.158), channel_id=1, source_target_pairs={{1,0},{2,1},{3,2},{4,3},{5,4},{6,5},{7,6},{8,7},{9,8},{10,9},{11,1... | collective-permute-start | bytes 589832 | tf_op jit(solution)/shard_map/ppermute | solution.py:190
  34.1 3.8 %fusion.89 = (f32[24,16,16,127]{3,2,1,0:T(8,128)}, f32[24,16,16,127]{3,2,1,0:T(8,128)}) fusion(f32[24,18,18,128]{3,2,1,0:T(8,128)S(1)} %broadcast_divide_fusion), kind=kLoop, calls=%fused_computation.139 | loop fusion | bytes 12484608 | tf_op jit(solution)/shard_map/jit(_roll_static)/slice | solution.py:213
  37.9 3.8 %fusion.90 = (f32[24,16,16,1]{3,2,1,0:T(8,128)}, f32[24,16,16,1]{3,2,1,0:T(8,128)}) fusion(f32[24,18,18,128]{3,2,1,0:T(8,128)S(1)} %broadcast_divide_fusion), kind=kLoop, calls=%fused_computation.140 | loop fusion | bytes 98304 | tf_op jit(solution)/shard_map/jit(_roll_static)/slice | solution.py:213
  42.5 3.3 %collective-permute-done.12 = f32[1,16,128]{2,1,0:T(8,128)S(1)} collective-permute-done((f32[1,16,128]{2,1,0:T(8,128)S(1)}, f32[1,16,128]{2,1,0:T(8,128)S(1)}, u32[]{:S(2)}, u32[]{:S(2)}) %collective-permute-start.12) | collective-permute-done | bytes 8224 | tf_op jit(solution)/shard_map/ppermute | solution.py:203
  46.5 1.9 constant_dynamic-update-slice_fusion.1
  49.2 16.9 %fusion.38 = f32[24,16,16,128]{3,2,1,0:T(8,128)} fusion(f32[24,16,16,128]{3,2,1,0:T(8,128)} %param.18, f32[24,18,16,128]{3,2,1,0:T(8,128)} %constant_dynamic-update-slice_fusion, f32[24,16,1,128]{3,2,1,0:T(1,128)S(1)} %bitcast.154, f32[24,16,1,128]{3,2,1,0:T(1,128)S(1)} %bitcast.153, f32[24,1,16,128]{3,2,1,0:T(8,128)S(1)} %collective-permute-done.5, ...), kind=kLoop, calls=%fused_computation.54 | loop fusion | flops 35389440 | bytes 38928384 | tf_op jit(solution)/shard_map/add | solution.py:215
  66.0 6.6 %fusion.91 = (f32[24,16,16,1]{3,2,1,0:T(8,128)}, f32[24,16,16,1]{3,2,1,0:T(8,128)}) fusion(f32[24,16,16,128]{3,2,1,0:T(8,128)} %fusion.38), kind=kLoop, calls=%fused_computation.141 | loop fusion | bytes 98304 | tf_op jit(solution)/shard_map/jit(_roll_static)/slice | solution.py:214
  73.0 5.0 %collective-permute-start.10 = (f32[24,16,1,128]{3,1,2,0:T(8,128)S(1)}, f32[24,16,1,128]{3,1,2,0:T(8,128)S(1)}, u32[]{:S(2)}, u32[]{:S(2)}) collective-permute-start(f32[24,16,1,128]{3,1,2,0:T(8,128)S(1)} %bitcast.160), channel_id=1, source_target_pairs={{1,0},{2,1},{3,2},{4,3},{5,4},{6,5},{7,6},{8,7},{9,8},{10,9},{11,1... | collective-permute-start | bytes 589832 | tf_op jit(solution)/shard_map/ppermute | solution.py:190
  78.0 2.8 %collective-permute-start.8 = (f32[24,1,16,128]{3,2,1,0:T(8,128)S(1)}, f32[24,1,16,128]{3,2,1,0:T(8,128)S(1)}, u32[]{:S(2)}, u32[]{:S(2)}) collective-permute-start(f32[24,1,16,128]{3,2,1,0:T(8,128)S(1)} %get-tuple-element.21), channel_id=1, source_target_pairs={{16,0},{32,16},{48,32},{64,48},{80,64},{96,80},{112,96},{0,112},{1... | collective-permute-start | bytes 589832 | tf_op jit(solution)/shard_map/ppermute | solution.py:190
  80.9 3.7 %fusion.92 = (f32[24,16,16,127]{3,2,1,0:T(8,128)}, f32[24,16,16,127]{3,2,1,0:T(8,128)}) fusion(f32[24,16,16,128]{3,2,1,0:T(8,128)S(1)} %copy-done.2), kind=kLoop, calls=%fused_computation.142 | loop fusion | bytes 12484608 | tf_op jit(solution)/shard_map/jit(_roll_static)/slice | solution.py:214
  85.4 4.6 %collective-permute-done.9 = f32[24,1,16,128]{3,2,1,0:T(8,128)S(1)} collective-permute-done((f32[24,1,16,128]{3,2,1,0:T(8,128)S(1)}, f32[24,1,16,128]{3,2,1,0:T(8,128)S(1)}, u32[]{:S(2)}, u32[]{:S(2)}) %collective-permute-start.9) | collective-permute-done | bytes 196640 | tf_op jit(solution)/shard_map/ppermute | solution.py:189
  90.1 19.2 %fusion.23 = f32[24,16,16,128]{3,2,1,0:T(8,128)} fusion(f32[24,16,16,128]{3,2,1,0:T(8,128)} %fusion.38, f32[24,16,1,128]{3,2,1,0:T(1,128)S(1)} %bitcast.156, f32[24,1,16,128]{3,2,1,0:T(8,128)S(1)} %collective-permute-done.8, f32[24,1,16,128]{3,2,1,0:T(8,128)S(1)} %collective-permute-done.9, f32[24,16,1,128]{3,2,1,0:T(1,128)S(1)} %bitcast.155, ...), kind=kLoop, calls=%fused_computation.31 | loop fusion | flops 38535168 | bytes 35389440 | tf_op jit(solution)/shard_map/add | solution.py:215
  109.3 10.2 %copy.62 = f32[24,16,16,128]{0,3,2,1:T(8,128)} copy(f32[24,16,16,128]{3,2,1,0:T(8,128)} %fusion.23) | data formatting | bytes 6291456 | tf_op jit(solution)/shard_map/add | solution.py:215
  119.5 20.1 %gather_fusion = bf16[4096,24]{1,0:T(8,128)(2,1)} fusion(f32[24,32768]{0,1:T(8,128)} %bitcast.142, s32[4096]{0:T(1024)S(1)} %broadcast_clamp_fusion), kind=kCustom, calls=%fused_computation | custom fusion | bytes 409600 | tf_op jit(solution)/shard_map/jit(_take)/gather | solution.py:264
  139.6 1.6 copy.63
  141.2 20.6 %fusion.7 = bf16[32,800,128]{2,1,0:T(8,128)(2,1)} fusion(bf16[800,1600]{1,0:T(8,128)(2,1)S(1)} %copy-done, bf16[24,32,128]{2,0,1:T(8,128)(2,1)S(1)} %copy.63, pred[32,128]{1,0:T(8,128)(4,1)S(1)} %compare_and_fusion, bf16[1600,24]{0,1:T(8,128)(2,1)S(1)} %copy-done.9), kind=kOutput, calls=%fused_computation.14 | convolution fusion | flops 10849583104 | bytes 9391104 | tf_op jit(solution)/shard_map/gf,bfr->bgr/dot_general | solution.py:226
  161.8 7.1 %fusion.59 = bf16[32,128,24]{1,2,0:T(8,128)(2,1)S(1)} fusion(bf16[32,800,128]{2,1,0:T(8,128)(2,1)} %fusion.7, bf16[400,800]{1,0:T(8,128)(2,1)} %param.24, bf16[24,400]{1,0:T(8,128)(2,1)S(1)} %copy-done.10), kind=kOutput, calls=%fused_computation.93 | convolution fusion | flops 2708373504 | bytes 7409408 | tf_op jit(solution)/shard_map/sh,bhr->bsr/dot_general | solution.py:231
  169.6 31.6 %scatter_fusion = f32[24,32768]{0,1:T(8,128)} fusion(f32[24,32768]{0,1:T(8,128)} %bitcast.143, s32[4096]{0:T(1024)S(1)} %bitcast.162, f32[4096,24]{1,0:T(8,128)S(1)} %copy.65), kind=kCustom, calls=%fused_computation.1 | custom fusion | flops 98304 | bytes 1196032 | tf_op jit(solution)/shard_map/scatter-add | solution.py:270
  201.2 11.5 %copy.67 = f32[24,16,16,128]{3,2,1,0:T(8,128)} copy(f32[24,16,16,128]{0,3,2,1:T(8,128)} %bitcast.144) | data formatting | bytes 6291456
  212.9 21.9 %scatter_custom_fusion.1 = f32[32768]{0:T(1024)S(1)} fusion(s32[4096]{0:T(1024)S(1)} %bitcast.163, f32[4096]{0:T(1024)S(1)} %broadcast_select_fusion, f32[]{:T(128)} %constant.17.clone.1), kind=kCustom, calls=%fused_computation.121 | custom fusion | flops 4096 | bytes 131076 | tf_op jit(solution)/shard_map/scatter-add | solution.py:275
  234.8 1.8 fusion.74.src
  236.7 24.7 %poisson.1 = f32[3,256,128]{2,1,0:T(8,128)} custom-call(f32[256,128]{1,0:T(8,128)} %fusion.74.src, f32[3,256,128]{2,1,0:T(8,128)} %bitcast.145, f32[128,128]{1,0:T(8,128)} %constant.49.clone.fz, f32[128,128]{1,0:T(8,128)} %constant.50.clone.fx, f32[128,128]{1,0:T(8,128)} %constant.51.clone.fxt, f32[256,256]{1,0:T(8,128)} %constant.52.clone.fy, ...), custom_call_target="tpu_custom_call" | custom-call | tf_op jit(solution)/shard_map/poisson/pallas_call | solution.py:146
  261.4 1.8 copy.84
  (64 shorter events, 7.4 us)
Async XLA Ops:
  0.6 140.6 %copy-start = (bf16[800,1600]{1,0:T(8,128)(2,1)S(1)}, bf16[800,1600]{1,0:T(8,128)(2,1)}, u32[]{:S(2)}) copy-start(bf16[800,1600]{1,0:T(8,128)(2,1)} %param.23) | copy-start | bytes 7680004
  1.7 23.4 %collective-permute-start = (f32[1,16,1,128]{3,2,1,0:T(1,128)S(1)}, f32[1,16,1,128]{3,2,1,0:T(1,128)S(1)}, u32[]{:S(2)}, u32[]{:S(2)}) collective-permute-start(f32[1,16,1,128]{3,2,1,0:T(1,128)S(1)} %get-tuple-element.37), channel_id=1, source_target_pairs={{0,1},{1,2},{2,3},{3,4},{4,5},{5,6},{6,7},{7,8},{8,9},{9,10},{10,1... | collective-permute-start | bytes 24584 | tf_op jit(solution)/shard_map/ppermute | solution.py:189
  5.5 23.9 %collective-permute-start.1 = (f32[1,1,16,128]{3,2,1,0:T(8,128)S(1)}, f32[1,1,16,128]{3,2,1,0:T(8,128)S(1)}, u32[]{:S(2)}, u32[]{:S(2)}) collective-permute-start(f32[1,1,16,128]{3,2,1,0:T(8,128)S(1)} %get-tuple-element.35), channel_id=1, source_target_pairs={{0,16},{16,32},{32,48},{48,64},{64,80},{80,96},{96,112},{112,0},{1... | collective-permute-start | bytes 24584 | tf_op jit(solution)/shard_map/ppermute | solution.py:189
  8.4 24.5 %collective-permute-start.2 = (f32[1,1,16,128]{3,2,1,0:T(8,128)S(1)}, f32[1,1,16,128]{3,2,1,0:T(8,128)S(1)}, u32[]{:S(2)}, u32[]{:S(2)}) collective-permute-start(f32[1,1,16,128]{3,2,1,0:T(8,128)S(1)} %get-tuple-element.36), channel_id=1, source_target_pairs={{16,0},{32,16},{48,32},{64,48},{80,64},{96,80},{112,96},{0,112},{1... | collective-permute-start | bytes 24584 | tf_op jit(solution)/shard_map/ppermute | solution.py:190
  10.6 22.3 %collective-permute-start.3 = (f32[1,16,1,128]{3,2,1,0:T(1,128)S(1)}, f32[1,16,1,128]{3,2,1,0:T(1,128)S(1)}, u32[]{:S(2)}, u32[]{:S(2)}) collective-permute-start(f32[1,16,1,128]{3,2,1,0:T(1,128)S(1)} %get-tuple-element.38), channel_id=1, source_target_pairs={{1,0},{2,1},{3,2},{4,3},{5,4},{6,5},{7,6},{8,7},{9,8},{10,9},{11,1... | collective-permute-start | bytes 24584 | tf_op jit(solution)/shard_map/ppermute | solution.py:190
  11.7 7.5 %copy-start.3 = (f32[24,16,16,128]{3,2,1,0:T(8,128)S(1)}, f32[24,16,16,128]{3,2,1,0:T(8,128)}, u32[]{:S(2)}) copy-start(f32[24,16,16,128]{3,2,1,0:T(8,128)} %param.18) | copy-start | bytes 9437188
  11.7 34.1 %collective-permute-start.5 = (f32[24,1,16,128]{3,2,1,0:T(8,128)S(1)}, f32[24,1,16,128]{3,2,1,0:T(8,128)S(1)}, u32[]{:S(2)}, u32[]{:S(2)}) collective-permute-start(f32[24,1,16,128]{3,2,1,0:T(8,128)S(1)} %get-tuple-element.29), channel_id=1, source_target_pairs={{0,16},{16,32},{32,48},{48,64},{64,80},{80,96},{96,112},{112,0},{1... | collective-permute-start | bytes 589832 | tf_op jit(solution)/shard_map/ppermute | solution.py:189
  19.1 4.3 %copy-start.4 = (f32[3,16,16,128]{3,2,1,0:T(8,128)S(1)}, f32[3,16,16,128]{3,2,1,0:T(8,128)}, u32[]{:S(2)}) copy-start(f32[3,16,16,128]{3,2,1,0:T(8,128)} %param.21) | copy-start | bytes 1179652
  19.1 5.1 %copy-start.6 = (s32[1,1,4096]{2,1,0:T(1,128)S(1)}, s32[1,1,4096]{2,1,0:T(1,128)}, u32[]{:S(2)}) copy-start(s32[1,1,4096]{2,1,0:T(1,128)} %param.27) | copy-start | bytes 49156
  19.1 14.5 %copy-start.5 = (f32[16,16,128]{2,1,0:T(8,128)S(1)}, f32[16,16,128]{2,1,0:T(8,128)}, u32[]{:S(2)}) copy-start(f32[16,16,128]{2,1,0:T(8,128)} %param.19) | copy-start | bytes 393220
  19.1 14.6 %copy-start.7 = (f32[24]{0:T(128)S(1)}, f32[24]{0:T(128)}, u32[]{:S(2)}) copy-start(f32[24]{0:T(128)} %param.20) | copy-start | bytes 292
  25.1 23.4 %collective-permute-start.4 = (f32[24,1,16,128]{3,2,1,0:T(8,128)S(1)}, f32[24,1,16,128]{3,2,1,0:T(8,128)S(1)}, u32[]{:S(2)}, u32[]{:S(2)}) collective-permute-start(f32[24,1,16,128]{3,2,1,0:T(8,128)S(1)} %get-tuple-element.28), channel_id=1, source_target_pairs={{16,0},{32,16},{48,32},{64,48},{80,64},{96,80},{112,96},{0,112},{1... | collective-permute-start | bytes 589832 | tf_op jit(solution)/shard_map/ppermute | solution.py:190
  29.4 19.8 %collective-permute-start.6 = (f32[24,16,1,128]{3,1,2,0:T(8,128)S(1)}, f32[24,16,1,128]{3,1,2,0:T(8,128)S(1)}, u32[]{:S(2)}, u32[]{:S(2)}) collective-permute-start(f32[24,16,1,128]{3,1,2,0:T(8,128)S(1)} %bitcast.158), channel_id=1, source_target_pairs={{1,0},{2,1},{3,2},{4,3},{5,4},{6,5},{7,6},{8,7},{9,8},{10,9},{11,1... | collective-permute-start | bytes 589832 | tf_op jit(solution)/shard_map/ppermute | solution.py:190
  32.9 16.3 %collective-permute-start.7 = (f32[24,16,1,128]{3,1,2,0:T(8,128)S(1)}, f32[24,16,1,128]{3,1,2,0:T(8,128)S(1)}, u32[]{:S(2)}, u32[]{:S(2)}) collective-permute-start(f32[24,16,1,128]{3,1,2,0:T(8,128)S(1)} %bitcast.157), channel_id=1, source_target_pairs={{0,1},{1,2},{2,3},{3,4},{4,5},{5,6},{6,7},{7,8},{8,9},{9,10},{10,1... | collective-permute-start | bytes 589832 | tf_op jit(solution)/shard_map/ppermute | solution.py:189
  32.9 8.9 %collective-permute-start.13 = (f32[16,1,128]{2,1,0:T(1,128)S(1)}, f32[16,1,128]{2,1,0:T(1,128)S(1)}, u32[]{:S(2)}, u32[]{:S(2)}) collective-permute-start(f32[16,1,128]{2,1,0:T(1,128)S(1)} %slice.249), channel_id=1, source_target_pairs={{0,15},{1,0},{2,1},{3,2},{4,3},{5,4},{6,5},{7,6},{8,7},{9,8},{10,9... | collective-permute-start | bytes 24584 | tf_op jit(solution)/shard_map/ppermute | solution.py:203
  41.8 4.0 %collective-permute-start.12 = (f32[1,16,128]{2,1,0:T(8,128)S(1)}, f32[1,16,128]{2,1,0:T(8,128)S(1)}, u32[]{:S(2)}, u32[]{:S(2)}) collective-permute-start(f32[1,16,128]{2,1,0:T(8,128)S(1)} %slice_bitcast_fusion.1), channel_id=1, source_target_pairs={{0,112},{16,0},{32,16},{48,32},{64,48},{80,64},{96,80},{112,96},{1... | collective-permute-start | bytes 24584 | tf_op jit(solution)/shard_map/ppermute | solution.py:203
  66.0 6.6 %copy-start.2 = (f32[24,16,16,128]{3,2,1,0:T(8,128)S(1)}, f32[24,16,16,128]{3,2,1,0:T(8,128)}, u32[]{:S(2)}) copy-start(f32[24,16,16,128]{3,2,1,0:T(8,128)} %fusion.38) | copy-start | bytes 9437188
  73.0 11.7 %collective-permute-start.10 = (f32[24,16,1,128]{3,1,2,0:T(8,128)S(1)}, f32[24,16,1,128]{3,1,2,0:T(8,128)S(1)}, u32[]{:S(2)}, u32[]{:S(2)}) collective-permute-start(f32[24,16,1,128]{3,1,2,0:T(8,128)S(1)} %bitcast.160), channel_id=1, source_target_pairs={{1,0},{2,1},{3,2},{4,3},{5,4},{6,5},{7,6},{8,7},{9,8},{10,9},{11,1... | collective-permute-start | bytes 589832 | tf_op jit(solution)/shard_map/ppermute | solution.py:190
  78.0 6.7 %collective-permute-start.11 = (f32[24,16,1,128]{3,1,2,0:T(8,128)S(1)}, f32[24,16,1,128]{3,1,2,0:T(8,128)S(1)}, u32[]{:S(2)}, u32[]{:S(2)}) collective-permute-start(f32[24,16,1,128]{3,1,2,0:T(8,128)S(1)} %bitcast.159), channel_id=1, source_target_pairs={{0,1},{1,2},{2,3},{3,4},{4,5},{5,6},{6,7},{7,8},{8,9},{9,10},{10,1... | collective-permute-start | bytes 589832 | tf_op jit(solution)/shard_map/ppermute | solution.py:189
  78.0 7.5 %collective-permute-start.8 = (f32[24,1,16,128]{3,2,1,0:T(8,128)S(1)}, f32[24,1,16,128]{3,2,1,0:T(8,128)S(1)}, u32[]{:S(2)}, u32[]{:S(2)}) collective-permute-start(f32[24,1,16,128]{3,2,1,0:T(8,128)S(1)} %get-tuple-element.21), channel_id=1, source_target_pairs={{16,0},{32,16},{48,32},{64,48},{80,64},{96,80},{112,96},{0,112},{1... | collective-permute-start | bytes 589832 | tf_op jit(solution)/shard_map/ppermute | solution.py:190
  80.8 9.3 %collective-permute-start.9 = (f32[24,1,16,128]{3,2,1,0:T(8,128)S(1)}, f32[24,1,16,128]{3,2,1,0:T(8,128)S(1)}, u32[]{:S(2)}, u32[]{:S(2)}) collective-permute-start(f32[24,1,16,128]{3,2,1,0:T(8,128)S(1)} %get-tuple-element.20), channel_id=1, source_target_pairs={{0,16},{16,32},{32,48},{48,64},{64,80},{80,96},{96,112},{112,0},{1... | collective-permute-start | bytes 589832 | tf_op jit(solution)/shard_map/ppermute | solution.py:189
  109.3 31.9 %copy-start.9 = (bf16[1600,24]{0,1:T(8,128)(2,1)S(1)}, bf16[1600,24]{0,1:T(8,128)(2,1)}, u32[]{:S(2)}) copy-start(bf16[1600,24]{0,1:T(8,128)(2,1)} %param.22) | copy-start | bytes 230404
  141.2 20.6 %copy-start.10 = (bf16[24,400]{1,0:T(8,128)(2,1)S(1)}, bf16[24,400]{1,0:T(8,128)(2,1)}, u32[]{:S(2)}) copy-start(bf16[24,400]{1,0:T(8,128)(2,1)} %param.25) | copy-start | bytes 57604
  201.2 11.5 %copy-start.8 = (f32[24]{0:T(128)S(1)}, f32[24]{0:T(128)}, u32[]{:S(2)}) copy-start(f32[24]{0:T(128)} %param.26) | copy-start | bytes 292
  201.2 62.0 %copy-start.1 = (bf16[800,1600]{1,0:T(8,128)(2,1)S(1)}, bf16[800,1600]{1,0:T(8,128)(2,1)}, u32[]{:S(2)}) copy-start(bf16[800,1600]{1,0:T(8,128)(2,1)} %param.23) | copy-start | bytes 7680004
